TPU v7x, 256 devices: a whole 4x4x8 slice. The times are simulated.
256 devices in a mesh: pix: 256 (over z, y, x, core).
Axes of the slice: x: 4, y: 4, z: 8, core: 2. Of those that a mesh axis runs over, the one named last changes fastest.
Arguments:
- green: float32 [16384, 6144], P('pix'), may hold values from -200 to 200, as said below
- sketch: float32 [6144, 128], P('pix'), may hold values from -0.078125 to 0.078125
Outputs:
- basis: float32 [16384, 128], P('pix')
- projection: float32 [6144, 128], P('pix')
- spectrum_gram: float32 [128, 128], replicated
Inputs may be any that keep to these rules, and one draw needn't show every extreme that they name: `green`: finite real entries; each patch's column has its own scale.
All inputs are finite; a program needn't handle non-finite values.
Results may differ from a plain program's by a relative error of at most 0.000086.
Values sent between devices are 32-bit elements; how exact they have to be, the bound alone decides.
A program may use at most 64 MiB of HBM per device.

v0:
```python
import jax
import jax.numpy as jnp
from jax import lax
from jax.sharding import Mesh
from jax.sharding import PartitionSpec as P

PATCHES = 6144
PIX = ("pix_0", "pix_1", "pix_2", "pix_3")


def in_order(tiles, dim):
    tiles = jnp.moveaxis(tiles, 0, dim)
    dims = tiles.shape
    return tiles.reshape(*dims[:dim], dims[dim] * dims[dim + 1], *dims[dim + 2 :])


def stacked_from(shard, axes, sequence):
    tiles = shard[None]
    for k in sequence:
        tiles = lax.all_gather(tiles, axes[k], axis=0, tiled=True)
    carried = [lax.axis_size(axes[k]) for k in reversed(sequence)]
    tiles = tiles.reshape(*carried, *shard.shape)
    turned = sorted(range(len(sequence)), key=lambda place: sequence[len(sequence) - 1 - place])
    return tiles.transpose(*turned, *range(len(sequence), tiles.ndim)).reshape(-1, *shard.shape)


def whole_of(shard, axes, sequence, dim):
    return in_order(stacked_from(shard, axes, sequence), dim)


def rows_for(lines, size):
    spare = -len(lines) % size
    return jnp.pad(lines, [(0, spare)] + [(0, 0)] * (lines.ndim - 1))


def sent_to_all(shard, axis):
    size = lax.axis_size(axis)
    return lax.all_to_all(
        jnp.broadcast_to(shard[None], (size, *shard.shape)), axis, 0, 0, tiled=True
    )


def whole_of_2(shard, axes, dim):
    far, near = axes
    leading = sent_to_all(shard, far)
    tiles = jnp.swapaxes(sent_to_all(leading, near), 0, 1)
    return in_order(tiles.reshape(-1, *shard.shape), dim)


def in_blocks(shard, dim, size):
    before, after = (shard.shape[:dim], shard.shape[dim + 1 :])
    return jnp.moveaxis(shard.reshape(*before, size, -1, *after), dim, 0)


def summed_on_arrival(shard, axis, dim):
    tiles = in_blocks(shard, dim, lax.axis_size(axis))
    arrived = lax.all_to_all(tiles, axis, split_axis=0, concat_axis=0, tiled=True)
    return arrived.sum(axis=0)


def summed_rows(shard, axes, dim):
    far, near = axes
    own = summed_on_arrival(in_blocks(shard, dim, lax.axis_size(far)), near, dim + 1)
    return jnp.sum(lax.all_to_all(own, far, 0, 0, tiled=True), axis=0)


def total_of(shard, axes):
    lines = shard.reshape(-1)
    padded = rows_for(lines, lax.axis_size(axes[0]) * lax.axis_size(axes[1]))
    whole = whole_of_2(summed_rows(padded, axes, 0), axes, 0)
    return lax.slice_in_dim(whole, 0, len(lines)).reshape(shard.shape)


def body(green, sketch):
    highest = lax.Precision.HIGHEST
    rows_here = green.shape[0]
    devices_pix = lax.axis_size(PIX)
    total_pixels = rows_here * devices_pix
    columns = green
    sketched = jnp.dot(
        columns,
        whole_of(sketch, PIX, (1, 0, 2, 3), 0),
        precision=highest,
        preferred_element_type=jnp.float32,
    )
    local_gram = jnp.dot(
        sketched.T, sketched, precision=highest, preferred_element_type=jnp.float32
    )
    gram = total_of(local_gram, (("pix_0", "pix_1"), ("pix_2", "pix_3")))
    lower = jnp.linalg.cholesky(gram)
    orthonormal = jax.scipy.linalg.solve_triangular(lower, sketched.T, lower=True).T
    columns = green
    projection = summed_rows(
        lax.dot_general(
            columns,
            orthonormal,
            (((0,), (0,)), ((), ())),
            precision=highest,
            preferred_element_type=jnp.float32,
        ),
        (("pix_0", "pix_1"), ("pix_2", "pix_3")),
        0,
    )
    basis = jnp.sqrt(jnp.float32(total_pixels)) * orthonormal
    local_spec = jnp.dot(
        projection.T, projection, precision=highest, preferred_element_type=jnp.float32
    )
    spectrum_gram = total_of(local_spec, (("pix_0", "pix_1"), ("pix_2", "pix_3"))) / jnp.float32(
        PATCHES
    )
    return (basis, projection, spectrum_gram)


def solution(mesh):
    split = Mesh(mesh.devices.reshape(8, 4, 4, 2), ("pix_0", "pix_1", "pix_2", "pix_3"))
    in_specs = (P(PIX, None), P(PIX, None))
    out_specs = (P(PIX, None), P(PIX, None), P())
    return jax.shard_map(body, mesh=split, in_specs=in_specs, out_specs=out_specs, check_vma=False)
```

profile of v0, /device:TPU:1, one launch (start us, length us, event | category | flops | bytes accessed | tf_op | source)
XLA Modules:
  0.0 305.1 jit_solution(14893671459518702312)
XLA Ops:
  7.2 10.7 %all-gather = f32[96,128]{1,0:T(8,128)S(1)} all-gather(f32[24,128]{1,0:T(8,128)} %param.3), channel_id=2, replica_groups=mesh['pix_0'=8,'pix_1'=4,'pix_2'=4,'pix_3'=2] {'pix_1'}, dimensions={0}, use_global_device_ids=true | all-gather | bytes 61440 | tf_op jit(solution)/shard_map/all_gather | solution.py:20
  17.9 24.3 %all_gather.13 = f32[32,24,128]{2,1,0:T(8,128)} all-gather(f32[4,24,128]{2,1,0:T(8,128)S(1)} %bitcast.49), channel_id=1, replica_groups=mesh['pix_0'=8,'pix_1'=4,'pix_2'=4,'pix_3'=2] {'pix_0'}, dimensions={0}, use_global_device_ids=true | all-gather | bytes 442368 | tf_op jit(solution)/shard_map/all_gather | solution.py:20
  42.3 36.8 %all-gather.4.cloned.1.call-done = f32[128,24,128]{2,1,0:T(8,128)} async-done(((f32[32,24,128]{2,1,0:T(8,128)}), f32[128,24,128]{2,1,0:T(8,128)}) %all-gather.4.cloned.1.call-update) | async-done | bytes 1572880 | tf_op jit(solution)/shard_map/all_gather | solution.py:20
  79.1 20.2 %all-gather.6.cloned.1.call-done = f32[256,24,128]{2,1,0:T(8,128)} async-done(((f32[128,24,128]{2,1,0:T(8,128)}), f32[256,24,128]{2,1,0:T(8,128)}) %all-gather.6.cloned.1.call-update) | async-done | bytes 3145744 | tf_op jit(solution)/shard_map/all_gather | solution.py:20
  99.3 2.3 copy.26
  101.6 2.1 fusion.4
  104.2 8.9 %all_to_all.60 = f32[8,1,2048]{2,1,0:T(1,128)S(1)} all-to-all(f32[8,1,2048]{2,1,0:T(1,128)S(1)} %reshape.47), channel_id=1, replica_groups=mesh['pix_0'=8,'pix_1'=4,'pix_2'=4,'pix_3'=2] {'pix_2','pix_3'}, dimensions={0} | all-to-all | bytes 131072 | tf_op jit(solution)/shard_map/all_to_all | solution.py:57
  113.5 0.7 reduce.8
  114.4 18.0 %all_to_all.61 = f32[32,1,64]{2,1,0:T(1,128)S(1)} all-to-all(f32[32,1,64]{2,1,0:T(1,128)S(1)} %bitcast.50), channel_id=1, replica_groups=mesh['pix_0'=8,'pix_1'=4,'pix_2'=4,'pix_3'=2] {'pix_0','pix_1'}, dimensions={0} | all-to-all | bytes 16384 | tf_op jit(solution)/shard_map/all_to_all | solution.py:64
  132.4 11.6 %all_to_all.62 = f32[32,1,64]{2,1,0:T(1,128)S(1)} all-to-all(f32[32,1,64]{2,1,0:T(1,128)S(1)} %broadcast_in_dim.17), channel_id=1, replica_groups=mesh['pix_0'=8,'pix_1'=4,'pix_2'=4,'pix_3'=2] {'pix_0','pix_1'}, dimensions={0} | all-to-all | bytes 16384 | tf_op jit(solution)/shard_map/all_to_all | solution.py:38
  144.2 10.6 %all_to_all.63 = f32[8,1,2048]{2,1,0:T(1,128)S(1)} all-to-all(f32[8,1,2048]{2,1,0:T(1,128)S(1)} %reshape.49), channel_id=1, replica_groups=mesh['pix_0'=8,'pix_1'=4,'pix_2'=4,'pix_3'=2] {'pix_2','pix_3'}, dimensions={0} | all-to-all | bytes 131072 | tf_op jit(solution)/shard_map/all_to_all | solution.py:38
  154.7 0.7 reduce.9
  155.9 11.7 %cholesky.16 = f32[128,128]{1,0:T(8,128)S(1)} custom-call(f32[128,128]{1,0:T(8,128)S(1)} %fusion.3), custom_call_target="Cholesky" | custom-call | tf_op jit(solution)/shard_map/jit(cholesky)/cholesky | solution.py:90
  167.6 0.6 compare_reduce_fusion
  168.2 0.7 fusion
  168.9 9.8 %custom-call.7 = f32[1,128,128]{1,2,0:T(8,128)S(1)} custom-call(f32[1,128,128]{2,1,0:T(8,128)S(1)} %fusion), custom_call_target="InvertDiagBlocksLowerTriangular" | custom-call | tf_op jit(solution)/shard_map/jit(_solve_triangular)/triangular_solve | solution.py:91
  178.9 4.3 %convolution_bitcast_fusion = f32[6144,128]{0,1:T(8,128)} fusion(f32[128,64]{0,1:T(8,128)S(1)} %fusion.1, f32[64,6144]{1,0:T(8,128)S(1)} %copy-done), kind=kOutput, calls=%fused_computation | convolution fusion | flops 603979776 | bytes 4751360 | tf_op jit(solution)/shard_map/dot_general | solution.py:94
  183.2 3.6 %copy.30 = f32[6144,128]{1,0:T(8,128)} copy(f32[6144,128]{0,1:T(8,128)} %convolution_bitcast_fusion) | data formatting | bytes 6291456 | tf_op jit(solution)/shard_map/dot_general | solution.py:94
  186.8 2.1 copy.31
  188.9 41.4 %all_to_all.64 = f32[8,32,24,128]{3,2,1,0:T(8,128)} all-to-all(f32[8,32,24,128]{3,2,1,0:T(8,128)S(1)} %copy.31), channel_id=1, replica_groups=mesh['pix_0'=8,'pix_1'=4,'pix_2'=4,'pix_3'=2] {'pix_2','pix_3'}, dimensions={0} | all-to-all | bytes 6291456 | tf_op jit(solution)/shard_map/all_to_all | solution.py:57
  230.3 2.1 reduce_sum.56
  232.4 16.5 %all_to_all.65 = f32[32,24,128]{2,1,0:T(8,128)S(1)} all-to-all(f32[32,24,128]{2,1,0:T(8,128)S(1)} %reduce_sum.56), channel_id=1, replica_groups=mesh['pix_0'=8,'pix_1'=4,'pix_2'=4,'pix_3'=2] {'pix_0','pix_1'}, dimensions={0} | all-to-all | bytes 786432 | tf_op jit(solution)/shard_map/all_to_all | solution.py:64
  249.5 10.0 %all_to_all.66 = f32[8,1,2048]{2,1,0:T(1,128)S(1)} all-to-all(f32[8,1,2048]{2,1,0:T(1,128)S(1)} %reshape.51), channel_id=1, replica_groups=mesh['pix_0'=8,'pix_1'=4,'pix_2'=4,'pix_3'=2] {'pix_2','pix_3'}, dimensions={0} | all-to-all | bytes 131072 | tf_op jit(solution)/shard_map/all_to_all | solution.py:57
  259.4 0.7 reduce.10
  260.3 12.4 %all_to_all.67 = f32[32,1,64]{2,1,0:T(1,128)S(1)} all-to-all(f32[32,1,64]{2,1,0:T(1,128)S(1)} %bitcast.52), channel_id=1, replica_groups=mesh['pix_0'=8,'pix_1'=4,'pix_2'=4,'pix_3'=2] {'pix_0','pix_1'}, dimensions={0} | all-to-all | bytes 16384 | tf_op jit(solution)/shard_map/all_to_all | solution.py:64
  272.8 11.6 %all_to_all.68 = f32[32,1,64]{2,1,0:T(1,128)S(1)} all-to-all(f32[32,1,64]{2,1,0:T(1,128)S(1)} %broadcast_in_dim.37), channel_id=1, replica_groups=mesh['pix_0'=8,'pix_1'=4,'pix_2'=4,'pix_3'=2] {'pix_0','pix_1'}, dimensions={0} | all-to-all | bytes 16384 | tf_op jit(solution)/shard_map/all_to_all | solution.py:38
  284.4 0.8 reshape.53
  285.1 6.6 %all-to-all-start.9 = ((f32[8,1,2048]{2,1,0:T(1,128)}), f32[8,1,2048]{2,1,0:T(1,128)S(1)}, u32[]{:S(2)}, u32[]{:S(2)}) async-start(f32[8,1,2048]{2,1,0:T(1,128)} %reshape.53), calls=%async_computation.9 | async-start | bytes 131072 | tf_op jit(solution)/shard_map/all_to_all | solution.py:38
  291.7 0.6 multiply_bitcast_fusion.1
  292.3 4.3 %all-to-all-done.9 = f32[8,1,2048]{2,1,0:T(1,128)S(1)} async-done(((f32[8,1,2048]{2,1,0:T(1,128)}), f32[8,1,2048]{2,1,0:T(1,128)S(1)}, u32[]{:S(2)}, u32[]{:S(2)}) %all-to-all-start.9) | async-done | bytes 65568 | tf_op jit(solution)/shard_map/all_to_all | solution.py:38
  296.6 0.7 reduce.11
  297.5 0.7 div.23
  (39 shorter events, 2.9 us)
Async XLA Ops:
  7.2 94.4 %copy-start = (f32[64,6144]{1,0:T(8,128)S(1)}, f32[64,6144]{1,0:T(8,128)}, u32[]{:S(2)}) copy-start(f32[64,6144]{1,0:T(8,128)} %param.2) | copy-start | bytes 4718596
  7.2 71.9 %all-gather.4.cloned.1.call-start = ((), (), s32[]{:S(2)}) async-start(), calls=%async_computation.10 | async-start | bytes 1966080 | tf_op jit(solution)/shard_map/all_gather | solution.py:20
  42.3 57.0 %all-gather.6.cloned.1.call-start = ((), (), s32[]{:S(2)}) async-start(), calls=%async_computation.11 | async-start | bytes 4718592 | tf_op jit(solution)/shard_map/all_gather | solution.py:20
  248.9 49.3 %copy-start.1 = (f32[24,128]{1,0:T(8,128)}, f32[24,128]{1,0:T(8,128)S(1)}, u32[]{:S(2)}) copy-start(f32[24,128]{1,0:T(8,128)S(1)} %reduce_sum.57) | copy-start | bytes 36868
  285.1 11.5 %all-to-all-start.9 = ((f32[8,1,2048]{2,1,0:T(1,128)}), f32[8,1,2048]{2,1,0:T(1,128)S(1)}, u32[]{:S(2)}, u32[]{:S(2)}) async-start(f32[8,1,2048]{2,1,0:T(1,128)} %reshape.53), calls=%async_computation.9 | async-start | bytes 131072 | tf_op jit(solution)/shard_map/all_to_all | solution.py:38
Sparse Core Ops, SparseCore 0:
  42.4 36.6 all-gather.3
  80.9 18.3 all-gather.5
where the time goes:
time: 306 us; the launch traced here: 305 us
  blocking collectives  176 us (58%)
  waiting for transfers between devices  61.2 us (20%)
  other arithmetic  28.7 us (9%)
  between operations  14.3 us (5%)
  local copies, waits for them, and re-layouts  11.3 us (4%)
  matrix products  7.14 us (2%)
  starting transfers between devices  6.69 us (2%)
    all_to_all x3, blocking collectives, summed_on_arrival(): lax.all_to_all(tiles, axis, split_axis=0, concat_axis=0, tiled=True)  60.2 us
    all_gather x2, waiting for transfers between devices, stacked_from(): tiles = lax.all_gather(tiles, axes[k], axis=0, tiled=True)  56.9 us
    all_to_all x3, blocking collectives, summed_rows(): return jnp.sum(lax.all_to_all(own, far, 0, 0, tiled=True), axis=0)  46.9 us
    all_gather x2, blocking collectives, stacked_from(): tiles = lax.all_gather(tiles, axes[k], axis=0, tiled=True)  35 us
    all_to_all x3, blocking collectives, sent_to_all(): lax.all_to_all(jnp.broadcast_to(shard[None], (size, *shard.shape)), axis,...  33.8 us
    another operation x3, other arithmetic, body(): lower = jnp.linalg.cholesky(gram)  12.4 us
    another operation x2, other arithmetic, body(): jax.scipy.linalg.solve_triangular(lower, sketched.T, lower=True)  10.5 us
    all_to_all x1, starting transfers between devices, sent_to_all(): lax.all_to_all(jnp.broadcast_to(shard[None], (size, *shard.shape)), axis,...  6.61 us
  transfers between devices with their start and end apart: 3, of which 3 were waited for; matrix products, arithmetic and copies ran while one was open for 0% of the time, Pallas kernels for 0%

commit v1 on v0

v1 whole, which is shorter than its diff:
```python
import jax
import jax.numpy as jnp
from jax import lax
from jax.experimental import pallas as pl
from jax.experimental.pallas import tpu as pltpu
from jax.sharding import Mesh
from jax.sharding import PartitionSpec as P

MESH = pl.DeviceIdType.MESH
HIGHEST = lax.Precision.HIGHEST
F32 = jnp.float32
PATCHES, RANK, PIXELS = 6144, 128, 16384
NZ, NY, NX, NC = 8, 4, 4, 2
ROWS = PIXELS // (NZ * NY * NX * NC)
OWN = PATCHES // (NZ * NY * NX * NC)
PAIR = NC * OWN
HALF = PATCHES // 2
HZ = NZ // 2
PLANE = NY * NX
STRIP = 384


def dot(a, b, dims):
    return lax.dot_general(a, b, (dims, ((), ())), precision=HIGHEST, preferred_element_type=F32)


def ring(v, k, n):
    return lax.rem(v + (k % n), n)


def comm_kernel(
    green,
    sketch,
    y_out,
    b_out,
    gram_out,
    t_out,
    gg,
    om,
    ypart,
    yother,
    ychip,
    bp,
    rs1,
    rs2a,
    rs2b,
    rf1,
    rf2a,
    rf2b,
    zb,
    part,
    rsbuf,
    zbuf,
    local_sem,
    pair_send,
    pair_recv,
    agz_send,
    agz_recv,
    ag_send,
    ag_recv,
    rs_send,
    rs_recv,
    rz_send,
    rz_recv,
    ar_send,
    ar_recv,
):
    z, y, x, c = (lax.axis_index(a) for a in "zyxc")
    other = (z, y, x, 1 - c)

    def remote(src, dst, ssem, rsem, to):
        return pltpu.make_async_remote_copy(
            src_ref=src, dst_ref=dst, send_sem=ssem, recv_sem=rsem, device_id=to, device_id_type=MESH
        )

    def arrived(dst, sem):
        pltpu.make_async_copy(dst, dst, sem).wait()

    own_rows = pl.ds(pl.multiple_of(c * ROWS, ROWS), ROWS)
    mine = pltpu.make_async_copy(
        green.at[:, pl.ds(pl.multiple_of(c * HALF, HALF), HALF)], gg.at[own_rows], local_sem
    )
    mine.start()

    partners = [
        (z, ring(y, dy, NY), ring(x, dx, NX), ring(c, dc, NC))
        for dy in range(NY)
        for dx in range(NX)
        for dc in range(NC)
        if dy or dx or dc
    ] + [(ring(z, dz, NZ), y, x, ring(c, dc, NC)) for dz in range(1, NZ) for dc in range(NC)]
    barrier = pltpu.get_barrier_semaphore()
    for to in partners:
        pl.semaphore_signal(barrier, inc=1, device_id=to, device_id_type=MESH)
    pl.semaphore_wait(barrier, len(partners))

    cz = z // HZ
    zl = lax.rem(z, HZ)
    shard = om.at[zl, y, x, pl.ds(pl.multiple_of(c * OWN, OWN), OWN)]
    agz = []
    for k in range(1, NZ):
        cp = remote(sketch, shard, agz_send.at[k], agz_recv.at[zl, c], (ring(z, k, NZ), y, x, cz))
        cp.start()
        agz.append(cp)
    to_pair = remote(sketch, shard, agz_send.at[0], agz_recv.at[zl, c], other)
    to_self = pltpu.make_async_copy(sketch, shard, agz_recv.at[zl, c])

    @pl.when(cz == c)
    def _():
        to_self.start()

    @pl.when(cz != c)
    def _():
        to_pair.start()

    give = remote(
        green.at[:, pl.ds(pl.multiple_of((1 - c) * HALF, HALF), HALF)],
        gg.at[own_rows],
        pair_send.at[0],
        pair_recv.at[0],
        other,
    )
    give.start()

    sends = []

    def place(col, f, s):
        return (s, f) if col == 0 else (f, s)

    f0 = (x, y)
    s0 = (y, x)

    def f_to(col, d):
        yy, xx = place(col, ring(f0[col], d, 4), s0[col])
        return (z, yy, xx, c)

    def s_to(col, d):
        yy, xx = place(col, f0[col], ring(s0[col], d, 4))
        return (z, yy, xx, c)

    def tile(buf, col, df, ds):
        yy, xx = place(col, ring(f0[col], df, 4), ring(s0[col], ds, 4))
        return buf.at[pl.ds(2 * col, 2), yy, xx]

    def half(buf, col, h, df, ds):
        yy, xx = place(col, ring(f0[col], df, 4), ring(s0[col], ds, 4))
        return buf.at[2 * col + h, yy, xx]

    def ag(col, n, ref, to):
        cp = remote(ref, ref, ag_send.at[col, n], ag_recv.at[col, n], to)
        cp.start()
        sends.append(cp)

    for zz in range(HZ):
        for cc in range(NC):
            arrived(om.at[zz, y, x, pl.ds(cc * OWN, OWN)], agz_recv.at[zz, cc])
    QS = (0, -1, 1, 2)
    for col in range(2):
        ag(col, 0, tile(om, col, 0, 0), f_to(col, 1))
        ag(col, 1, tile(om, col, 0, 0), f_to(col, -1))
    for col in range(2):
        ag(col, 4, tile(om, col, 0, 0), s_to(col, 1))
        ag(col, 5, tile(om, col, 0, 0), s_to(col, -1))
    for col in range(2):
        arrived(tile(om, col, -1, 0), ag_recv.at[col, 0])
        ag(col, 2, half(om, col, 0, -1, 0), f_to(col, 1))
        ag(col, 6, tile(om, col, -1, 0), s_to(col, 1))
        ag(col, 7, tile(om, col, -1, 0), s_to(col, -1))
        arrived(tile(om, col, 1, 0), ag_recv.at[col, 1])
        ag(col, 3, half(om, col, 1, 1, 0), f_to(col, -1))
        ag(col, 8, tile(om, col, 1, 0), s_to(col, 1))
        ag(col, 9, tile(om, col, 1, 0), s_to(col, -1))
    for q in range(4):
        for col in range(2):
            if q == 1:
                arrived(half(om, col, 0, 2, 0), ag_recv.at[col, 2])
                arrived(half(om, col, 1, 2, 0), ag_recv.at[col, 3])
                ag(col, 10, tile(om, col, 2, 0), s_to(col, 1))
                ag(col, 11, tile(om, col, 2, 0), s_to(col, -1))
            arrived(tile(om, col, QS[q], -1), ag_recv.at[col, 4 + 2 * q])
            ag(col, 12 + 2 * q, half(om, col, 0, QS[q], -1), s_to(col, 1))
            arrived(tile(om, col, QS[q], 1), ag_recv.at[col, 5 + 2 * q])
            ag(col, 13 + 2 * q, half(om, col, 1, QS[q], 1), s_to(col, -1))
    for q in range(4):
        for col in range(2):
            arrived(half(om, col, 0, QS[q], 2), ag_recv.at[col, 12 + 2 * q])
            arrived(half(om, col, 1, QS[q], 2), ag_recv.at[col, 13 + 2 * q])

    mine.wait()
    give.wait_recv()
    acc = jnp.zeros((NC * ROWS, RANK), F32)
    per = HALF // STRIP
    ys = NY // 2
    for k in range(per):
        rows = om[k // 2, pl.ds(ys * (k % 2), ys)].reshape(STRIP, RANK)
        acc = acc + dot(gg[:, k * STRIP : (k + 1) * STRIP], rows, ((1,), (0,)))
    ypart[...] = acc
    swap = remote(ypart, yother, pair_send.at[1], pair_recv.at[1], other)
    swap.start()
    swap.wait_recv()
    ychip[...] = ypart[...] + yother[...]
    yown = ychip[own_rows, :]
    y_out[...] = yown

    me = (y * NX + x) * NC + c
    piece = pl.ds(pl.multiple_of(8 * (y * NX + x), 8), 8)

    def ar_scatter(n):
        for dy in range(NY):
            for dx in range(NX):
                for dc in range(NC):
                    if dy or dx or dc:
                        yy, xx, cc = ring(y, dy, NY), ring(x, dx, NX), ring(c, dc, NC)
                        rows = pl.ds(pl.multiple_of(8 * (yy * NX + xx), 8), 8)
                        k = (dy * NX + dx) * NC + dc
                        cp = remote(
                            part.at[n, rows],
                            rsbuf.at[n, me],
                            ar_send.at[n, k],
                            ar_recv.at[n, k],
                            (z, yy, xx, cc),
                        )
                        cp.start()
                        sends.append(cp)
        rsbuf[n, me] = part[n, piece, :]

    def ar_sum(n):
        for dy in range(NY):
            for dx in range(NX):
                for dc in range(NC):
                    if dy or dx or dc:
                        src = (ring(y, -dy, NY) * NX + ring(x, -dx, NX)) * NC + ring(c, -dc, NC)
                        k = (dy * NX + dx) * NC + dc
                        arrived(rsbuf.at[n, src], ar_recv.at[n, k])
        zbuf[n, z] = jnp.sum(rsbuf[n], axis=0)
        for dz in range(1, NZ):
            cp = remote(
                zbuf.at[n, z], zbuf.at[n, z], ar_send.at[n, 31 + dz], ar_recv.at[n, 31 + dz], (ring(z, dz, NZ), y, x, c)
            )
            cp.start()
            sends.append(cp)

    def ar_gather(n, out):
        for dz in range(1, NZ):
            arrived(zbuf.at[n, ring(z, -dz, NZ)], ar_recv.at[n, 31 + dz])
        out[piece, :] = jnp.sum(zbuf[n], axis=0)
        for dy in range(NY):
            for dx in range(NX):
                if dy or dx:
                    k = 39 + dy * NX + dx
                    cp = remote(
                        out.at[piece],
                        out.at[piece],
                        ar_send.at[n, k],
                        ar_recv.at[n, k],
                        (z, ring(y, dy, NY), ring(x, dx, NX), c),
                    )
                    cp.start()
                    sends.append(cp)

    def ar_done(n, out):
        for dy in range(NY):
            for dx in range(NX):
                if dy or dx:
                    k = 39 + dy * NX + dx
                    src = ring(y, -dy, NY) * NX + ring(x, -dx, NX)
                    rows = pl.ds(pl.multiple_of(8 * src, 8), 8)
                    arrived(out.at[rows], ar_recv.at[n, k])

    part[0] = dot(yown, yown, ((0,), (0,)))
    ar_scatter(0)

    for k in range(per):
        res = dot(gg[:, k * STRIP : (k + 1) * STRIP], ychip[...], ((0,), (0,)))
        bp[k // 2, pl.ds(ys * (k % 2), ys)] = res.reshape(ys, NX, PAIR, RANK)

    def rs(col, n, src, dst, to):
        cp = remote(src, dst, rs_send.at[col, n], rs_recv.at[col, n], to)
        cp.start()
        sends.append(cp)

    RQ = (2, -1, 1, 0)
    for q in range(4):
        for col in range(2):
            rs(col, 2 * q, half(bp, col, 0, RQ[q], 2), rs1.at[col, q, 0], s_to(col, 1))
            rs(col, 2 * q + 1, half(bp, col, 1, RQ[q], 2), rs1.at[col, q, 1], s_to(col, -1))
            rs(col, 8 + 2 * q, half(bp, col, 1, RQ[q], 1), rs2a.at[col, q, 0], s_to(col, 1))
            rs(col, 9 + 2 * q, half(bp, col, 0, RQ[q], -1), rs2a.at[col, q, 1], s_to(col, -1))

    def add(dst, *srcs):
        tot = dst[...]
        for s in srcs:
            tot = tot + s[...]
        dst[...] = tot

    def s_forward(q, col):
        arrived(rs1.at[col, q, 0], rs_recv.at[col, 2 * q])
        blk = half(bp, col, 0, RQ[q], 1)
        add(blk, rs1.at[col, q, 0])
        rs(col, 16 + 2 * q, blk, rs2b.at[col, q, 0], s_to(col, 1))
        arrived(rs1.at[col, q, 1], rs_recv.at[col, 2 * q + 1])
        blk = half(bp, col, 1, RQ[q], -1)
        add(blk, rs1.at[col, q, 1])
        rs(col, 17 + 2 * q, blk, rs2b.at[col, q, 1], s_to(col, -1))

    def s_finish(q, col):
        for d in range(2):
            arrived(rs2a.at[col, q, d], rs_recv.at[col, 8 + 2 * q + d])
            arrived(rs2b.at[col, q, d], rs_recv.at[col, 16 + 2 * q + d])
        add(half(bp, col, 0, RQ[q], 0), rs2b.at[col, q, 0], rs2a.at[col, q, 1])
        add(half(bp, col, 1, RQ[q], 0), rs2a.at[col, q, 0], rs2b.at[col, q, 1])
        if q == 0:
            rs(col, 24, half(bp, col, 0, 2, 0), rf1.at[col, 0], f_to(col, 1))
            rs(col, 25, half(bp, col, 1, 2, 0), rf1.at[col, 1], f_to(col, -1))
        if q == 1:
            rs(col, 27, half(bp, col, 0, -1, 0), rf2a.at[col, 1], f_to(col, -1))
        if q == 2:
            rs(col, 26, half(bp, col, 1, 1, 0), rf2a.at[col, 0], f_to(col, 1))
            arrived(rf1.at[col, 0], rs_recv.at[col, 24])
            blk = half(bp, col, 0, 1, 0)
            add(blk, rf1.at[col, 0])
            rs(col, 28, blk, rf2b.at[col, 0], f_to(col, 1))
            arrived(rf1.at[col, 1], rs_recv.at[col, 25])
            blk = half(bp, col, 1, -1, 0)
            add(blk, rf1.at[col, 1])
            rs(col, 29, blk, rf2b.at[col, 1], f_to(col, -1))

    for q in range(4):
        for col in range(2):
            s_forward(q, col)
        if q == 1:
            ar_sum(0)
    for q in range(4):
        for col in range(2):
            s_finish(q, col)
        if q == 1:
            ar_gather(0, gram_out)
    for col in range(2):
        for d in range(2):
            arrived(rf2a.at[col, d], rs_recv.at[col, 26 + d])
            arrived(rf2b.at[col, d], rs_recv.at[col, 28 + d])
        add(half(bp, col, 0, 0, 0), rf2b.at[col, 0], rf2a.at[col, 1])
        add(half(bp, col, 1, 0, 0), rf2a.at[col, 0], rf2b.at[col, 1])

    for zz in range(HZ):
        for cc in range(NC):
            k = zz * NC + cc
            zt = c * HZ + zz
            src = bp.at[zz, y, x, pl.ds(cc * OWN, OWN)]
            here = jnp.logical_and(zt == z, c == cc)
            far = remote(src, zb.at[z], rz_send.at[k], rz_recv.at[z], (zt, y, x, cc))
            near = pltpu.make_async_copy(src, zb.at[z], rz_recv.at[z])

            @pl.when(here)
            def _():
                near.start()

            @pl.when(jnp.logical_not(here))
            def _():
                far.start()

    ar_done(0, gram_out)
    for k in range(NZ):
        arrived(zb.at[k], rz_recv.at[k])
    b = jnp.sum(zb[...], axis=0)
    eye = lax.broadcasted_iota(jnp.int32, (RANK, RANK), 0) == lax.broadcasted_iota(jnp.int32, (RANK, RANK), 1)
    diag = jnp.sum(jnp.where(eye, gram_out[...], 0.0), axis=0, keepdims=True)
    b = b * lax.rsqrt(diag)
    b_out[...] = b
    part[1] = dot(b, b, ((0,), (0,)))
    ar_scatter(1)
    ar_sum(1)
    ar_gather(1, t_out)
    ar_done(1, t_out)

    for cp in agz:
        cp.wait_send()

    @pl.when(cz != c)
    def _():
        to_pair.wait_send()

    give.wait_send()
    swap.wait_send()
    for cp in sends:
        cp.wait_send()
    for zz in range(HZ):
        for cc in range(NC):
            k = zz * NC + cc
            zt = c * HZ + zz
            src = bp.at[zz, y, x, pl.ds(cc * OWN, OWN)]

            @pl.when(jnp.logical_not(jnp.logical_and(zt == z, c == cc)))
            def _():
                remote(src, zb.at[z], rz_send.at[k], rz_recv.at[z], (zt, y, x, cc)).wait_send()


def communicate(green, sketch):
    vm = pltpu.VMEM
    dma = pltpu.SemaphoreType.DMA
    blk = (HZ, NY, NX, PAIR, RANK)
    return pl.pallas_call(
        comm_kernel,
        name="comm",
        out_shape=[
            jax.ShapeDtypeStruct((ROWS, RANK), F32),
            jax.ShapeDtypeStruct((OWN, RANK), F32),
            jax.ShapeDtypeStruct((RANK, RANK), F32),
            jax.ShapeDtypeStruct((RANK, RANK), F32),
        ],
        in_specs=[pl.BlockSpec(memory_space=pl.ANY), pl.BlockSpec(memory_space=vm)],
        out_specs=[pl.BlockSpec(memory_space=vm)] * 4,
        scratch_shapes=[
            vm((NC * ROWS, HALF), F32),
            vm(blk, F32),
            vm((NC * ROWS, RANK), F32),
            vm((NC * ROWS, RANK), F32),
            vm((NC * ROWS, RANK), F32),
            vm(blk, F32),
            vm((2, 4, 2, PAIR, RANK), F32),
            vm((2, 4, 2, PAIR, RANK), F32),
            vm((2, 4, 2, PAIR, RANK), F32),
            vm((2, 2, PAIR, RANK), F32),
            vm((2, 2, PAIR, RANK), F32),
            vm((2, 2, PAIR, RANK), F32),
            vm((NZ, OWN, RANK), F32),
            vm((2, RANK, RANK), F32),
            vm((2, PLANE * NC, 8, RANK), F32),
            vm((2, NZ, 8, RANK), F32),
            dma,
            dma((2,)),
            dma((2,)),
            dma((NZ,)),
            dma((HZ, NC)),
            dma((2, 20)),
            dma((2, 20)),
            dma((2, 30)),
            dma((2, 30)),
            dma((NZ,)),
            dma((NZ,)),
            dma((2, 55)),
            dma((2, 55)),
        ],
        compiler_params=pltpu.CompilerParams(collective_id=0, has_side_effects=True, vmem_limit_bytes=40 * 2**20),
    )(green, sketch)


def finish_kernel(ys, bs, gram, t, basis, projection, spectrum, a, m):
    eye = lax.broadcasted_iota(jnp.int32, (RANK, RANK), 0) == lax.broadcasted_iota(jnp.int32, (RANK, RANK), 1)
    g = gram[...]
    picked = jnp.where(eye, g, 0.0)
    across = lax.rsqrt(jnp.sum(picked, axis=0, keepdims=True))
    down = lax.rsqrt(jnp.sum(picked, axis=1, keepdims=True))
    a[...] = g * across * down
    m[...] = jnp.where(eye, 1.0, 0.0)
    sub = lax.broadcasted_iota(jnp.int32, (8, RANK), 0)
    for k in range(RANK // 8):
        p = a[8 * k : 8 * k + 8, :]
        q = m[8 * k : 8 * k + 8, :]
        cols = [jnp.broadcast_to(p[:, 8 * k + j : 8 * k + j + 1], (8, RANK)) for j in range(8)]
        for j in range(8):
            pivot = jnp.broadcast_to(cols[j][j : j + 1, :], (8, RANK))
            r = lax.rsqrt(pivot)
            r = r * (1.5 - 0.5 * pivot * r * r)
            below = sub > j
            mult = jnp.where(below, cols[j] * r, 0.0)
            prow = jnp.broadcast_to(p[j : j + 1, :], (8, RANK)) * r
            qrow = jnp.broadcast_to(q[j : j + 1, :], (8, RANK)) * r
            at = sub == j
            p = jnp.where(at, prow, p - mult * prow)
            q = jnp.where(at, qrow, q - mult * qrow)
            for l in range(j + 1, 8):
                cols[l] = cols[l] - mult * (jnp.broadcast_to(cols[l][j : j + 1, :], (8, RANK)) * r)
        m[8 * k : 8 * k + 8, :] = q
        if k < RANK // 8 - 1:
            rest = slice(8 * k + 8, RANK)
            lhs = p[:, 8 * k + 8 :]
            a[rest, :] = a[rest, :] - dot(lhs, p, ((0,), (0,)))
            m[rest, :] = m[rest, :] - dot(lhs, q, ((0,), (0,)))
    inv = m[...]
    basis[...] = 128.0 * dot(ys[...] * across, inv, ((1,), (1,)))
    projection[...] = dot(bs[...], inv, ((1,), (1,)))
    spectrum[...] = dot(dot(inv, t[...], ((1,), (0,))), inv, ((1,), (1,))) / float(PATCHES)


def body(green, sketch):
    ys, bs, gram, t = communicate(green, sketch)
    vm = pltpu.VMEM
    return pl.pallas_call(
        finish_kernel,
        name="finish",
        out_shape=[
            jax.ShapeDtypeStruct((ROWS, RANK), F32),
            jax.ShapeDtypeStruct((OWN, RANK), F32),
            jax.ShapeDtypeStruct((RANK, RANK), F32),
        ],
        in_specs=[pl.BlockSpec(memory_space=vm)] * 4,
        out_specs=[pl.BlockSpec(memory_space=vm)] * 3,
        scratch_shapes=[vm((RANK, RANK), F32), vm((RANK, RANK), F32)],
    )(ys, bs, gram, t)


def solution(mesh):
    axes = ("z", "y", "x", "c")
    split = Mesh(mesh.devices.reshape(NZ, NY, NX, NC), axes)
    in_specs = (P(axes, None), P(axes, None))
    out_specs = (P(axes, None), P(axes, None), P())
    return jax.shard_map(body, mesh=split, in_specs=in_specs, out_specs=out_specs, check_vma=False)
```

time: 306 us -> 88.8 us (0.29)
  blocking collectives: 176 us -> 0 us
  Pallas kernels: 0 us -> 83.4 us
  waiting for transfers between devices: 61.2 us -> 0 us
  other arithmetic: 28.7 us -> 0 us
  between operations: 14.3 us -> 0.66 us
  matrix products: 7.14 us -> 0 us
  local copies, waits for them, and re-layouts: 11.3 us -> 4.56 us
  starting transfers between devices: 6.69 us -> 0 us
    all_to_all x9 -> x0, blocking collectives: 141 us -> none  [the longest x3 60.2 us: summed_on_arrival(): lax.all_to_all(tiles, axis, split_axis=0, concat_axis=0, tiled=True)]
    pallas_call x0 -> x2, Pallas kernels: none -> 83.4 us  [the longest x1 72.5 us: communicate(): pl.pallas_call(comm_kernel, name='comm', out_shape=[jax.ShapeDtypeStruct(...]
    all_gather x2 -> x0, waiting for transfers between devices: 56.9 us -> none  [stacked_from(): tiles = lax.all_gather(tiles, axes[k], axis=0, tiled=True)]
    all_gather x2 -> x0, blocking collectives: 35 us -> none  [stacked_from(): tiles = lax.all_gather(tiles, axes[k], axis=0, tiled=True)]
    another operation x5 -> x0, other arithmetic: 22.9 us -> none  [the longest x3 12.4 us: body(): lower = jnp.linalg.cholesky(gram)]
    dot_general x4 -> x0, matrix products: 6.95 us -> none  [the longest x1 4.32 us: body(): lax.dot_general(columns, orthonormal, (((0,), (0,)), ((), ())), precision...]
    all_to_all x1 -> x0, starting transfers between devices: 6.61 us -> none  [sent_to_all(): lax.all_to_all(jnp.broadcast_to(shard[None], (size, *shard.shape)), axis,...]
    transpose x3 -> x0, local copies, waits for them, and re-layouts: 4.44 us -> none  [the longest x1 2.27 us: stacked_from(): tiles.transpose(*turned, *range(len(sequence), tiles.ndim))]
  transfers between devices with their start and end apart: 3 -> 0, of which waited for: 3 -> 0; matrix products, arithmetic and copies ran while one was open for 0% -> 0% of each run, Pallas kernels for 0% -> 0%
where the time goes in v1:
time: 88.8 us; the launch traced here: 88.6 us
  Pallas kernels  83.4 us (94%)
  local copies, waits for them, and re-layouts  4.56 us (5%)
    pallas_call x1, Pallas kernels, communicate(): pl.pallas_call(comm_kernel, name='comm', out_shape=[jax.ShapeDtypeStruct(...  72.5 us
    pallas_call x1, Pallas kernels, body(): pl.pallas_call(finish_kernel, name='finish', out_shape=[jax.ShapeDtypeStr...  10.9 us
    unnamed x12, local copies, waits for them, and re-layouts  4.56 us

profile of v1, /device:TPU:1, one launch (start us, length us, event | category | flops | bytes accessed | tf_op | source)
XLA Modules:
  0.0 88.6 jit_solution(10783965076220543743)
XLA Ops:
  0.6 0.0 copy-start
  0.6 1.4 %copy-done = f32[64,6144]{1,0:T(8,128)S(1)} copy-done((f32[64,6144]{1,0:T(8,128)S(1)}, f32[64,6144]{1,0:T(8,128)}, u32[]{:S(2)}) %copy-start) | copy-done | bytes 1572888
  2.0 0.0 copy-start.4
  2.0 0.7 copy-done.4
  2.7 72.5 %comm.1 = (f32[64,128]{1,0:T(8,128)S(1)}, f32[24,128]{1,0:T(8,128)S(1)}, f32[128,128]{1,0:T(8,128)S(1)}, f32[128,128]{1,0:T(8,128)S(1)}) custom-call(f32[64,6144]{1,0:T(8,128)S(1)} %copy-done, f32[24,128]{1,0:T(8,128)S(1)} %copy-done.4), custom_call_target="tpu_custom_call" | custom-call | tf_op jit(solution)/shard_map/comm/pallas_call | solution.py:402
  75.2 0.0 copy-start.1
  75.2 0.6 copy-done.1
  75.9 0.0 copy-start.2
  75.9 0.6 copy-done.2
  76.5 0.0 copy-start.3
  76.5 0.6 copy-done.3
  77.1 0.0 copy-start.5
  77.1 0.6 copy-done.5
  77.7 10.9 %finish.1 = (f32[64,128]{1,0:T(8,128)}, f32[24,128]{1,0:T(8,128)}, f32[128,128]{1,0:T(8,128)}) custom-call(f32[64,128]{1,0:T(8,128)} %copy-done.3, f32[24,128]{1,0:T(8,128)} %copy-done.5, f32[128,128]{1,0:T(8,128)} %copy-done.1, f32[128,128]{1,0:T(8,128)} %copy-done.2), custom_call_target="tpu_custom_call" | custom-call | tf_op jit(solution)/shard_map/finish/pallas_call | solution.py:489
Async XLA Ops:
  0.6 1.4 %copy-start = (f32[64,6144]{1,0:T(8,128)S(1)}, f32[64,6144]{1,0:T(8,128)}, u32[]{:S(2)}) copy-start(f32[64,6144]{1,0:T(8,128)} %green.1) | copy-start | bytes 4718596
  2.0 0.7 copy-start.4
  75.2 0.6 copy-start.1
  75.9 0.6 copy-start.2
  76.5 0.6 copy-start.3
  77.1 0.6 copy-start.5
